TPU v7x, 128 devices: a whole 4x4x4 slice. The times are simulated.
128 devices in a mesh: rows: 32 (over y, x, core), cols: 4 (over z).
Axes of the slice: x: 4, y: 4, z: 4, core: 2. Of those that a mesh axis runs over, the one named last changes fastest.
Arguments:
- token_ids: int32 [64, 2048], P('rows', 'cols'), may hold values from 0 to 524287, as said below
- lengths: int32 [64], P('rows'), may hold values from 1 to 2048
- table: bfloat16 [524288, 512], P('rows', 'cols'), may hold values from -6 to 6
- attn_gain: float32 [512], replicated, may hold values from 0.1 to 1.9
- w_qkv: bfloat16 [512, 1536], replicated, may hold values from -2 to 2
- w_out: bfloat16 [512, 512], replicated, may hold values from -0.25 to 0.25
- mlp_gain: float32 [512], replicated, may hold values from 0.1 to 1.9
- w_in: bfloat16 [512, 4096], replicated, may hold values from -0.25 to 0.25
- w_down: bfloat16 [2048, 512], replicated, may hold values from -0.125 to 0.125
Outputs:
- layer_out: bfloat16 [64, 2048, 512], P('rows', 'cols')
Inputs may be any that keep to these rules, and one draw needn't show every extreme that they name: `token_ids`: ids lie in 0 to 524287. In each aligned block of 2 histories (4096 positions) at most 341 ids fall in any one block of 16384 consecutive table rows, and in every such block of histories some block of table rows receives exactly 341.
All inputs are finite; a program needn't handle non-finite values.
Results may differ from a plain program's by a relative error of at most 0.012.
Values may be sent and summed in bfloat16 or wider, within the bound.
No kernel may reach another device: no remote copies, remote signals or barrier semaphores. Data moves between devices by JAX's collectives and lax.ppermute only.
A program may use at most 192 MiB of HBM per device.

v0:
```python
import jax
import jax.numpy as jnp
from jax import lax
from jax.sharding import PartitionSpec as P

D = 512
HEADS = 8
FF = 2048


def in_order(blocks, dim):
    blocks = jnp.moveaxis(blocks, 0, dim)
    dims = blocks.shape
    return blocks.reshape(*dims[:dim], dims[dim] * dims[dim + 1], *dims[dim + 2 :])


def sent_to_all(shard, axis):
    copies = jnp.broadcast_to(shard, (lax.axis_size(axis), *shard.shape))
    return lax.all_to_all(copies, axis, split_axis=0, concat_axis=0, tiled=True)


def gathered_copies(shard, axis, dim):
    return in_order(sent_to_all(shard, axis), dim)


def rms_norm(values_f32, gain):
    mean_sq = jnp.mean(values_f32 * values_f32, axis=-1, keepdims=True)
    return values_f32 * lax.rsqrt(mean_sq + 1e-06) * gain


def local(token_ids, lengths, table, attn_gain, w_qkv, w_out, mlp_gain, w_in, w_down):
    batch_dev, quarter = token_ids.shape
    col_count = lax.axis_size("cols")
    row_count = lax.axis_size("rows")
    full_len = quarter * col_count
    block_rows, col_width = table.shape
    zero_bf = jnp.zeros((), jnp.bfloat16)
    own_ids = gathered_copies(token_ids, "cols", 1)
    flat_ids = own_ids.reshape(-1)
    token_count = flat_ids.shape[0]
    capacity = 8 * token_count // (3 * row_count)
    owner_block = flat_ids // block_rows
    onehot = (owner_block[:, None] == jnp.arange(row_count, dtype=jnp.int32)[None, :]).astype(
        jnp.int32
    )
    slot_rank = jnp.sum((jnp.cumsum(onehot, axis=0) - 1) * onehot, axis=1)
    slot_index = owner_block * capacity + slot_rank
    requests = jnp.full((row_count * capacity,), -1, jnp.int32)
    requests = (
        requests.at[slot_index]
        .set(flat_ids - owner_block * block_rows)
        .reshape(row_count, capacity)
    )
    asked = lax.all_to_all(requests, "rows", split_axis=0, concat_axis=0, tiled=True)
    looked = jnp.take(table, jnp.maximum(asked, 0), axis=0)
    looked = jnp.where((asked >= 0)[..., None], looked, zero_bf)
    returned = lax.all_to_all(looked, "rows", split_axis=0, concat_axis=0, tiled=True)
    embedded = returned.reshape(row_count * capacity, col_width)[slot_index]
    embedded = embedded.reshape(batch_dev, full_len, col_width)
    sequence = lax.all_to_all(embedded, "cols", split_axis=1, concat_axis=2, tiled=True)
    residual = sequence.astype(jnp.float32)
    normed = rms_norm(residual, attn_gain).astype(jnp.bfloat16)
    projected = jnp.einsum("bqe,ef->bqf", normed, w_qkv, preferred_element_type=jnp.float32).astype(
        jnp.bfloat16
    )
    head_dim = D // HEADS
    queries = projected[..., :D].reshape(batch_dev, quarter, HEADS, head_dim)
    keys = projected[..., D : 2 * D]
    values = projected[..., 2 * D :]
    query_pos = lax.axis_index("cols") * quarter + jnp.arange(quarter, dtype=jnp.int32)
    running_max = jnp.full((batch_dev, HEADS, quarter), -1e30, jnp.float32)
    key_piece = lax.all_gather(keys, "cols", axis=1, tiled=True)
    value_piece = lax.all_gather(values, "cols", axis=1, tiled=True)
    piece_len = key_piece.shape[1]
    key_heads = key_piece.reshape(batch_dev, piece_len, HEADS, head_dim)
    value_heads = value_piece.reshape(batch_dev, piece_len, HEADS, head_dim)
    scores = (
        jnp.einsum("bqhd,bkhd->bhqk", queries, key_heads, preferred_element_type=jnp.float32)
        * 0.125
    )
    key_pos = jnp.arange(piece_len, dtype=jnp.int32)
    causal = key_pos[None, :] <= query_pos[:, None]
    inside = key_pos[None, :] < lengths[:, None]
    valid = causal[None, None, :, :] & inside[:, None, None, :]
    scores = jnp.where(valid, scores, -1e30)
    new_max = jnp.maximum(running_max, jnp.max(scores, axis=-1))
    probs = jnp.where(valid, jnp.exp(scores - new_max[..., None]), 0.0)
    running_sum = jnp.sum(probs, axis=-1)
    weighted = jnp.einsum(
        "bhqk,bkhd->bhqd",
        probs.astype(jnp.bfloat16),
        value_heads,
        preferred_element_type=jnp.float32,
    )
    final_max, final_sum, weighted = (new_max, running_sum, weighted)
    summed = weighted / final_sum[..., None]
    attended = (
        jnp.transpose(summed, (0, 2, 1, 3)).reshape(batch_dev, quarter, D).astype(jnp.bfloat16)
    )
    hidden = (
        residual + jnp.einsum("bqe,ef->bqf", attended, w_out, preferred_element_type=jnp.float32)
    ).astype(jnp.bfloat16)
    hidden_f32 = hidden.astype(jnp.float32)
    normed_two = rms_norm(hidden_f32, mlp_gain).astype(jnp.bfloat16)
    gate_up = jnp.einsum("bqe,ef->bqf", normed_two, w_in, preferred_element_type=jnp.float32)
    act = (jax.nn.silu(gate_up[..., :FF]) * gate_up[..., FF:]).astype(jnp.bfloat16)
    return (
        hidden_f32 + jnp.einsum("bqf,fe->bqe", act, w_down, preferred_element_type=jnp.float32)
    ).astype(jnp.bfloat16)


def solution(mesh):
    in_specs = (P("rows", "cols"), P("rows"), P("rows", "cols"), P(), P(), P(), P(), P(), P())
    out_specs = P("rows", "cols", None)
    return jax.shard_map(local, mesh=mesh, in_specs=in_specs, out_specs=out_specs, check_vma=False)
```

profile of v0, /device:TPU:1, one launch (start us, length us, event | category | flops | bytes accessed | tf_op | source)
XLA Modules:
  0.0 354.8 jit_solution(12214605746236327788)
XLA Ops:
  6.5 0.0 copy-start
  6.5 0.8 broadcast_in_dim.67
  7.4 9.8 %all_to_all.28 = s32[4,2,512]{2,1,0:T(2,128)S(1)} all-to-all(s32[4,2,512]{2,1,0:T(2,128)S(1)} %broadcast_in_dim.67), channel_id=1, replica_groups=mesh['rows'=32,'cols'=4] {'cols'}, dimensions={0} | all-to-all | bytes 32768 | tf_op jit(solution)/shard_map/all_to_all | solution.py:19
  17.3 0.1 fusion.33
  17.4 9.2 %reduce-window.6 = s32[32,32,128]{2,1,0:T(8,128)S(1)} reduce-window(s32[32,32,128]{2,1,0:T(8,128)S(1)} %fusion.33, s32[]{:T(128)} %constant.29.clone.1), window={size=1x1x128 pad=0_0x0_0x127_0}, to_apply=%region_0.1 | reduce-window | flops 16646144 | bytes 1048580 | tf_op jit(solution)/shard_map/reduce-window
  26.6 0.8 slice_reduce_fusion
  27.4 0.2 reduce-window.9
  27.6 0.2 add_add_fusion
  27.8 0.3 fusion.31
  28.2 0.1 compare_select_fusion
  28.3 15.5 %scatter_custom_fusion = s32[10912]{0:T(1024)S(1)} fusion(s32[4096]{0:T(1024)S(1)} %bitcast.80, s32[4096]{0:T(1024)S(1)} %get-tuple-element.10, s32[]{:T(128)} %constant.27.clone.1), kind=kCustom, calls=%fused_computation.65 | custom fusion | bytes 43652 | tf_op jit(solution)/shard_map/scatter | solution.py:51
  43.8 0.2 all_to_all.20
  44.0 16.3 %all_to_all.29 = s32[32,1,341]{2,1,0:T(1,128)S(1)} all-to-all(s32[32,1,341]{2,1,0:T(1,128)S(1)} %all_to_all.20), channel_id=1, replica_groups=mesh['rows'=32,'cols'=4] {'rows'}, dimensions={0} | all-to-all | bytes 87296 | tf_op jit(solution)/shard_map/all_to_all | solution.py:54
  60.3 0.1 reshape.255
  60.4 23.7 %gather_fusion = bf16[10912,128]{1,0:T(8,128)(2,1)} fusion(bf16[16384,128]{1,0:T(8,128)(2,1)} %param.11, s32[11264]{0:T(1024)S(1)} %pad_clamp_fusion), kind=kCustom, calls=%fused_computation | custom fusion | bytes 5630592 | tf_op jit(solution)/shard_map/jit(_take)/gather | solution.py:55
  84.1 4.4 %reshape.254 = bf16[32,341,128]{2,1,0:T(8,128)(2,1)} reshape(bf16[10912,128]{1,0:T(8,128)(2,1)} %gather_fusion) | data formatting | bytes 5586944 | tf_op jit(solution)/shard_map/jit(_take)/gather | solution.py:55
  88.6 6.0 %select_select_fusion = bf16[32,341,128]{2,1,0:T(8,128)(2,1)} fusion(bf16[32,341,128]{2,1,0:T(8,128)(2,1)} %reshape.254, pred[32,341]{1,0:T(8,128)(4,1)S(1)} %get-tuple-element.9, pred[32,341]{1,0:T(8,128)(4,1)S(1)} %get-tuple-element.8), kind=kLoop, calls=%fused_computation.21 | loop fusion | flops 2793472 | bytes 5608768 | tf_op jit(solution)/shard_map/jit(_where)/select_n | solution.py:56
  94.6 4.8 %all-to-all-start.2 = ((bf16[32,341,128]{2,1,0:T(8,128)(2,1)}), bf16[32,341,128]{2,1,0:T(8,128)(2,1)}, u32[]{:S(2)}, u32[]{:S(2)}) async-start(bf16[32,341,128]{2,1,0:T(8,128)(2,1)} %select_select_fusion), calls=%async_computation.2 | async-start | bytes 5636096 | tf_op jit(solution)/shard_map/all_to_all | solution.py:57
  99.4 0.0 all-gather.3.cloned.1.call-start
  99.4 36.1 %all-to-all-done.2 = bf16[32,341,128]{2,1,0:T(8,128)(2,1)} async-done(((bf16[32,341,128]{2,1,0:T(8,128)(2,1)}), bf16[32,341,128]{2,1,0:T(8,128)(2,1)}, u32[]{:S(2)}, u32[]{:S(2)}) %all-to-all-start.2) | async-done | bytes 2793504 | tf_op jit(solution)/shard_map/all_to_all | solution.py:57
  135.5 4.4 %reshape.246 = bf16[10912,128]{1,0:T(8,128)(2,1)} reshape(bf16[32,341,128]{2,1,0:T(8,128)(2,1)} %all-to-all-done.2) | data formatting | bytes 5586944 | tf_op jit(solution)/shard_map/reshape | solution.py:58
  139.9 13.2 %gather_fusion.1 = bf16[4096,128]{1,0:T(8,128)(2,1)S(1)} fusion(bf16[10912,128]{1,0:T(8,128)(2,1)} %reshape.246, s32[4096]{0:T(1024)S(1)} %broadcast_clamp_fusion), kind=kCustom, calls=%fused_computation.1 | custom fusion | bytes 2113536 | tf_op jit(solution)/shard_map/gather | solution.py:58
  153.1 8.7 %copy.63 = bf16[2,2048,128]{2,0,1:T(2,128)(2,1)S(1)} copy(bf16[2,2048,128]{2,1,0:T(8,128)(2,1)S(1)} %bitcast.73) | data formatting | bytes 2097152 | tf_op jit(solution)/shard_map/reshape | solution.py:59
  161.8 15.0 %all_to_all.30 = bf16[2,2048,128]{2,0,1:T(2,128)(2,1)S(1)} all-to-all(bf16[2,2048,128]{2,0,1:T(2,128)(2,1)S(1)} %copy.63), channel_id=1, replica_groups=mesh['rows'=32,'cols'=4] {'cols'}, dimensions={1} | all-to-all | bytes 2097152 | tf_op jit(solution)/shard_map/all_to_all | solution.py:60
  176.8 0.0 copy-start.2
  176.8 1.5 copy_convert_fusion
  178.2 2.9 copy.65
  181.2 0.6 multiply_reduce_fusion
  181.9 0.0 copy-done.2
  181.9 1.8 fusion.18
  183.7 3.2 convolution_convert_fusion
  187.0 0.0 copy-start.3
  187.0 1.7 fusion.44
  188.6 0.0 all-gather.3.cloned.1.call-update
  188.7 0.0 all-gather.5.cloned.1.call-start
  188.7 0.0 copy-done.3
  188.7 0.1 iota_compare_fusion.3
  188.8 0.7 iota_compare_fusion
  189.5 2.6 broadcast_and_fusion
  192.1 1.3 copy.67
  193.4 0.0 all-gather.5.cloned.1.call-update
  193.5 43.3 %all-gather.3.cloned.1.call-done = bf16[2,2048,512]{2,1,0:T(8,128)(2,1)} async-done(((bf16[2,512,512]{2,1,0:T(8,128)(2,1)}), bf16[2,2048,512]{2,1,0:T(8,128)(2,1)}) %all-gather.3.cloned.1.call-update) | async-done | bytes 4194320 | tf_op jit(solution)/shard_map/all_gather | solution.py:72
  236.7 6.3 %copy.68 = bf16[2,2048,512]{1,2,0:T(8,128)(2,1)} copy(bf16[2,2048,512]{2,1,0:T(8,128)(2,1)} %all-gather.3.cloned.1.call-done) | data formatting | bytes 8388608 | tf_op jit(solution)/shard_map/all_gather | solution.py:72
  243.0 0.0 copy-start.1
  243.0 27.9 %fusion = (f32[2,8,512]{2,1,0:T(8,128)S(1)}, f32[2,8,512,2048]{3,2,1,0:T(8,128)}) fusion(pred[2,512,2048]{2,1,0:T(8,128)(4,1)} %broadcast_and_fusion, bf16[2,512,8,64]{1,3,2,0:T(8,128)(2,1)} %bitcast.72, bf16[2,2048,8,64]{1,3,2,0:T(8,128)(2,1)} %bitcast.70), kind=kOutput, calls=%fused_computation.5 | convolution fusion | flops 2197807104 | bytes 74481664 | tf_op jit(solution)/shard_map/bqhd,bkhd->bhqk/dot_general | solution.py:78
  271.0 0.0 copy-done.1
  271.0 22.5 %fusion.1 = f32[2,8,512]{2,1,0:T(8,128)S(1)} fusion(f32[2,8,512,2048]{3,2,1,0:T(8,128)} %get-tuple-element.15, f32[2,8,512]{2,1,0:T(8,128)S(1)} %broadcast_maximum_fusion, pred[2,512,2048]{2,1,0:T(8,128)(4,1)S(1)} %copy-done.1), kind=kLoop, calls=%fused_computation.6 | loop fusion | flops 83877888 | bytes 69271552 | tf_op jit(solution)/shard_map/reduce_sum | solution.py:88
  293.4 0.0 all-gather.5.cloned.1.call-done
  293.5 6.3 %copy.69 = bf16[2,2048,512]{1,2,0:T(8,128)(2,1)} copy(bf16[2,2048,512]{2,1,0:T(8,128)(2,1)} %all-gather.5.cloned.1.call-done) | data formatting | bytes 8388608 | tf_op jit(solution)/shard_map/all_gather | solution.py:73
  299.8 27.0 %fusion.16 = bf16[2,512,8,64]{1,3,2,0:T(8,128)(2,1)S(1)} fusion(bf16[2,2048,8,64]{1,3,2,0:T(8,128)(2,1)} %bitcast.74, f32[2,8,512,2048]{3,2,1,0:T(8,128)} %get-tuple-element.15, f32[2,8,512]{2,1,0:T(8,128)S(1)} %broadcast_maximum_fusion, pred[2,512,2048]{2,1,0:T(8,128)(4,1)} %broadcast_and_fusion, f32[2,512,8]{1,2,0:T(8,128)S(1)} %bitcast.84), kind=kOutput, calls=%fused_computation.28 | convolution fusion | flops 2232418304 | bytes 74514432 | tf_op jit(solution)/shard_map/bhqk,bkhd->bhqd/dot_general | solution.py:89
  326.7 0.0 copy-start.4
  326.8 0.0 copy-start.5
  326.8 2.7 fusion.11
  329.5 0.3 copy-done.4
  329.7 0.0 copy-done.5
  329.7 8.3 %fusion.7 = f32[2,512,4096]{2,1,0:T(8,128)} fusion(bf16[512,4096]{1,0:T(8,128)(2,1)S(1)} %copy-done.4, bf16[2,512,512]{1,2,0:T(8,128)(2,1)S(1)} %get-tuple-element.17, f32[512]{0:T(512)S(1)} %copy-done.5, f32[2,512]{1,0:T(2,128)S(1)} %add_rsqrt_fusion), kind=kOutput, calls=%fused_computation.12 | convolution fusion | flops 4297064448 | bytes 22026240 | tf_op jit(solution)/shard_map/bqe,ef->bqf/dot_general | solution.py:105
  338.1 0.0 copy-done
  338.1 8.6 %fusion.14 = bf16[2,512,512]{1,2,0:T(8,128)(2,1)S(1)} fusion(bf16[2,512,512]{1,2,0:T(8,128)(2,1)S(1)} %get-tuple-element.17, bf16[2048,512]{1,0:T(8,128)(2,1)S(1)} %copy-done, f32[2,512,4096]{2,1,0:T(8,128)} %fusion.7), kind=kOutput, calls=%fused_computation.25 | convolution fusion | flops 2161639424 | bytes 20971520 | tf_op jit(solution)/shard_map/bqf,fe->bqe/dot_general | solution.py:108
  346.6 1.3 copy.74
  (16 shorter events, 0.2 us)
Async XLA Ops:
  6.5 331.5 %copy-start = (bf16[2048,512]{1,0:T(8,128)(2,1)S(1)}, bf16[2048,512]{1,0:T(8,128)(2,1)}, u32[]{:S(2)}) copy-start(bf16[2048,512]{1,0:T(8,128)(2,1)} %param.17) | copy-start | bytes 6291460
  94.6 40.9 %all-to-all-start.2 = ((bf16[32,341,128]{2,1,0:T(8,128)(2,1)}), bf16[32,341,128]{2,1,0:T(8,128)(2,1)}, u32[]{:S(2)}, u32[]{:S(2)}) async-start(bf16[32,341,128]{2,1,0:T(8,128)(2,1)} %select_select_fusion), calls=%async_computation.2 | async-start | bytes 5636096 | tf_op jit(solution)/shard_map/all_to_all | solution.py:57
  99.4 137.4 %all-gather.3.cloned.1.call-start = ((), (), s32[]{:S(2)}) async-start(), calls=%async_computation.4 | async-start | bytes 5242880 | tf_op jit(solution)/shard_map/all_gather | solution.py:72
  176.8 5.1 %copy-start.2 = (f32[512]{0:T(512)S(1)}, f32[512]{0:T(512)}, u32[]{:S(2)}) copy-start(f32[512]{0:T(512)} %param.12) | copy-start | bytes 6148
  187.0 1.8 copy-start.3
  188.7 104.8 %all-gather.5.cloned.1.call-start = ((), (), s32[]{:S(2)}) async-start(), calls=%async_computation.5 | async-start | bytes 5242880 | tf_op jit(solution)/shard_map/all_gather | solution.py:73
  243.0 27.9 %copy-start.1 = (pred[2,512,2048]{2,1,0:T(8,128)(4,1)S(1)}, pred[2,512,2048]{2,1,0:T(8,128)(4,1)}, u32[]{:S(2)}) copy-start(pred[2,512,2048]{2,1,0:T(8,128)(4,1)} %broadcast_and_fusion) | copy-start | bytes 6291460
  326.7 3.0 copy-start.4
  326.8 3.0 copy-start.5
Sparse Core Ops, SparseCore 0:
  188.8 47.9 all-gather.2
  238.4 48.5 all-gather.4
where the time goes:
time: 356 us; the launch traced here: 355 us
  local copies, waits for them, and re-layouts  92 us (26%)
  waiting for transfers between devices  79.4 us (22%)
  matrix products  77.7 us (22%)
  other arithmetic  46 us (13%)
  blocking collectives  41.1 us (12%)
  between operations  13.7 us (4%)
  starting transfers between devices  4.87 us (1%)
    all_gather x1, waiting for transfers between devices, local(): key_piece = lax.all_gather(keys, 'cols', axis=1, tiled=True)  43.3 us
    all_to_all x1, waiting for transfers between devices, local(): lax.all_to_all(looked, 'rows', split_axis=0, concat_axis=0, tiled=True)  36.1 us
    gather x2, local copies, waits for them, and re-layouts, local(): looked = jnp.take(table, jnp.maximum(asked, 0), axis=0)  28.1 us
    dot_general x1, matrix products, local(): jnp.einsum('bqhd,bkhd->bhqk', queries, key_heads, preferred_element_type=...  27.9 us
    dot_general x1, matrix products, local(): jnp.einsum('bhqk,bkhd->bhqd', probs.astype(jnp.bfloat16), value_heads, pr...  27 us
    reduce_sum x1, other arithmetic, local(): running_sum = jnp.sum(probs, axis=-1)  22.5 us
    all_to_all x1, blocking collectives, local(): lax.all_to_all(requests, 'rows', split_axis=0, concat_axis=0, tiled=True)  16.3 us
    scatter x1, local copies, waits for them, and re-layouts, local(): requests = requests.at[slot_index].set(flat_ids - owner_block * block_row...  15.5 us
  transfers between devices with their start and end apart: 3, of which 2 were waited for; matrix products, arithmetic and copies ran while one was open for 17% of the time, Pallas kernels for 0%

commit v1 on v0

--- a/solution.py
+++ b/solution.py
@@ -69,8 +69,11 @@
     values = projected[..., 2 * D :]
     query_pos = lax.axis_index("cols") * quarter + jnp.arange(quarter, dtype=jnp.int32)
     running_max = jnp.full((batch_dev, HEADS, quarter), -1e30, jnp.float32)
-    key_piece = lax.all_gather(keys, "cols", axis=1, tiled=True)
-    value_piece = lax.all_gather(values, "cols", axis=1, tiled=True)
+    key_piece, value_piece = jnp.split(
+        lax.all_gather(jnp.concatenate([keys, values], axis=0), "cols", axis=1, tiled=True),
+        [keys.shape[0]],
+        axis=0,
+    )
     piece_len = key_piece.shape[1]
     key_heads = key_piece.reshape(batch_dev, piece_len, HEADS, head_dim)
     value_heads = value_piece.reshape(batch_dev, piece_len, HEADS, head_dim)

time: 356 us -> 396 us (1.11)
  waiting for transfers between devices: 79.4 us -> 114 us
  local copies, waits for them, and re-layouts: 92 us -> 96.4 us
    all_gather x2 -> x1, waiting for transfers between devices: 43.3 us -> 78.2 us  [local(): lax.all_gather(jnp.concatenate([keys, values], axis=0), 'cols', axis=1, t...]
    split x0 -> x3, local copies, waits for them, and re-layouts: none -> 18.4 us  [local(): jnp.split(lax.all_gather(jnp.concatenate([keys, values], axis=0), 'cols',...]
    all_gather x2 -> x0, local copies, waits for them, and re-layouts: 12.6 us -> none  [the longest x1 6.29 us: local(): value_piece = lax.all_gather(values, 'cols', axis=1, tiled=True)]
  transfers between devices with their start and end apart: 3 -> 2, of which waited for: 2 -> 2; matrix products, arithmetic and copies ran while one was open for 17% -> 1% of each run, Pallas kernels for 0% -> 0%
where the time goes in v1:
time: 396 us; the launch traced here: 395 us
  waiting for transfers between devices  114 us (29%)
  local copies, waits for them, and re-layouts  96.4 us (24%)
  matrix products  77 us (19%)
  other arithmetic  47.5 us (12%)
  blocking collectives  41.1 us (10%)
  between operations  13.7 us (3%)
  starting transfers between devices  4.82 us (1%)
    all_gather x1, waiting for transfers between devices, local(): lax.all_gather(jnp.concatenate([keys, values], axis=0), 'cols', axis=1, t...  78.2 us
    all_to_all x1, waiting for transfers between devices, local(): lax.all_to_all(looked, 'rows', split_axis=0, concat_axis=0, tiled=True)  36.1 us
    gather x2, local copies, waits for them, and re-layouts, local(): looked = jnp.take(table, jnp.maximum(asked, 0), axis=0)  28.1 us
    dot_general x1, matrix products, local(): jnp.einsum('bhqk,bkhd->bhqd', probs.astype(jnp.bfloat16), value_heads, pr...  27.1 us
    dot_general x1, matrix products, local(): jnp.einsum('bqhd,bkhd->bhqk', queries, key_heads, preferred_element_type=...  27.1 us
    reduce_sum x1, other arithmetic, local(): running_sum = jnp.sum(probs, axis=-1)  22.4 us
    split x3, local copies, waits for them, and re-layouts, local(): jnp.split(lax.all_gather(jnp.concatenate([keys, values], axis=0), 'cols',...  18.4 us
    all_to_all x1, blocking collectives, local(): lax.all_to_all(requests, 'rows', split_axis=0, concat_axis=0, tiled=True)  16.3 us
  transfers between devices with their start and end apart: 2, of which 2 were waited for; matrix products, arithmetic and copies ran while one was open for 1% of the time, Pallas kernels for 0%

profile of v1, /device:TPU:1, one launch (start us, length us, event | category | flops | bytes accessed | tf_op | source)
XLA Modules:
  0.0 394.8 jit_solution(10793870791452522970)
XLA Ops:
  6.5 0.0 copy-start
  6.5 0.8 broadcast_in_dim.67
  7.4 9.8 %all_to_all.28 = s32[4,2,512]{2,1,0:T(2,128)S(1)} all-to-all(s32[4,2,512]{2,1,0:T(2,128)S(1)} %broadcast_in_dim.67), channel_id=1, replica_groups=mesh['rows'=32,'cols'=4] {'cols'}, dimensions={0} | all-to-all | bytes 32768 | tf_op jit(solution)/shard_map/all_to_all | solution.py:19
  17.3 0.1 fusion.33
  17.4 9.2 %reduce-window.6 = s32[32,32,128]{2,1,0:T(8,128)S(1)} reduce-window(s32[32,32,128]{2,1,0:T(8,128)S(1)} %fusion.33, s32[]{:T(128)} %constant.29.clone.1), window={size=1x1x128 pad=0_0x0_0x127_0}, to_apply=%region_0.1 | reduce-window | flops 16646144 | bytes 1048580 | tf_op jit(solution)/shard_map/reduce-window
  26.6 0.8 slice_reduce_fusion
  27.4 0.2 reduce-window.9
  27.6 0.2 add_add_fusion
  27.8 0.3 fusion.31
  28.2 0.1 compare_select_fusion
  28.3 15.5 %scatter_custom_fusion = s32[10912]{0:T(1024)S(1)} fusion(s32[4096]{0:T(1024)S(1)} %bitcast.81, s32[4096]{0:T(1024)S(1)} %get-tuple-element.12, s32[]{:T(128)} %constant.27.clone.1), kind=kCustom, calls=%fused_computation.66 | custom fusion | bytes 43652 | tf_op jit(solution)/shard_map/scatter | solution.py:51
  43.8 0.2 all_to_all.20
  44.0 16.3 %all_to_all.29 = s32[32,1,341]{2,1,0:T(1,128)S(1)} all-to-all(s32[32,1,341]{2,1,0:T(1,128)S(1)} %all_to_all.20), channel_id=1, replica_groups=mesh['rows'=32,'cols'=4] {'rows'}, dimensions={0} | all-to-all | bytes 87296 | tf_op jit(solution)/shard_map/all_to_all | solution.py:54
  60.3 0.1 reshape.255
  60.4 23.7 %gather_fusion = bf16[10912,128]{1,0:T(8,128)(2,1)} fusion(bf16[16384,128]{1,0:T(8,128)(2,1)} %param.11, s32[11264]{0:T(1024)S(1)} %pad_clamp_fusion), kind=kCustom, calls=%fused_computation | custom fusion | bytes 5630592 | tf_op jit(solution)/shard_map/jit(_take)/gather | solution.py:55
  84.1 4.4 %reshape.254 = bf16[32,341,128]{2,1,0:T(8,128)(2,1)} reshape(bf16[10912,128]{1,0:T(8,128)(2,1)} %gather_fusion) | data formatting | bytes 5586944 | tf_op jit(solution)/shard_map/jit(_take)/gather | solution.py:55
  88.6 6.0 %select_select_fusion = bf16[32,341,128]{2,1,0:T(8,128)(2,1)} fusion(bf16[32,341,128]{2,1,0:T(8,128)(2,1)} %reshape.254, pred[32,341]{1,0:T(8,128)(4,1)S(1)} %get-tuple-element.11, pred[32,341]{1,0:T(8,128)(4,1)S(1)} %get-tuple-element.10), kind=kLoop, calls=%fused_computation.21 | loop fusion | flops 2793472 | bytes 5608768 | tf_op jit(solution)/shard_map/jit(_where)/select_n | solution.py:56
  94.6 4.8 %all-to-all-start.2 = ((bf16[32,341,128]{2,1,0:T(8,128)(2,1)}), bf16[32,341,128]{2,1,0:T(8,128)(2,1)}, u32[]{:S(2)}, u32[]{:S(2)}) async-start(bf16[32,341,128]{2,1,0:T(8,128)(2,1)} %select_select_fusion), calls=%async_computation.2 | async-start | bytes 5636096 | tf_op jit(solution)/shard_map/all_to_all | solution.py:57
  99.4 0.0 all-gather.2.cloned.1.call-start
  99.4 36.1 %all-to-all-done.2 = bf16[32,341,128]{2,1,0:T(8,128)(2,1)} async-done(((bf16[32,341,128]{2,1,0:T(8,128)(2,1)}), bf16[32,341,128]{2,1,0:T(8,128)(2,1)}, u32[]{:S(2)}, u32[]{:S(2)}) %all-to-all-start.2) | async-done | bytes 2793504 | tf_op jit(solution)/shard_map/all_to_all | solution.py:57
  135.5 4.4 %reshape.246 = bf16[10912,128]{1,0:T(8,128)(2,1)} reshape(bf16[32,341,128]{2,1,0:T(8,128)(2,1)} %all-to-all-done.2) | data formatting | bytes 5586944 | tf_op jit(solution)/shard_map/reshape | solution.py:58
  139.9 13.2 %gather_fusion.1 = bf16[4096,128]{1,0:T(8,128)(2,1)S(1)} fusion(bf16[10912,128]{1,0:T(8,128)(2,1)} %reshape.246, s32[4096]{0:T(1024)S(1)} %broadcast_clamp_fusion), kind=kCustom, calls=%fused_computation.1 | custom fusion | bytes 2113536 | tf_op jit(solution)/shard_map/gather | solution.py:58
  153.1 8.7 %copy.63 = bf16[2,2048,128]{2,0,1:T(2,128)(2,1)S(1)} copy(bf16[2,2048,128]{2,1,0:T(8,128)(2,1)S(1)} %bitcast.74) | data formatting | bytes 2097152 | tf_op jit(solution)/shard_map/reshape | solution.py:59
  161.8 15.0 %all_to_all.30 = bf16[2,2048,128]{2,0,1:T(2,128)(2,1)S(1)} all-to-all(bf16[2,2048,128]{2,0,1:T(2,128)(2,1)S(1)} %copy.63), channel_id=1, replica_groups=mesh['rows'=32,'cols'=4] {'cols'}, dimensions={1} | all-to-all | bytes 2097152 | tf_op jit(solution)/shard_map/all_to_all | solution.py:60
  176.8 0.0 copy-start.2
  176.8 0.6 multiply_reduce_fusion
  177.5 1.5 copy_convert_fusion
  179.0 2.9 copy.65
  181.9 0.0 copy-done.2
  181.9 1.8 fusion.18
  183.7 3.2 convolution_convert_fusion
  186.9 0.2 fusion.45
  187.2 0.0 copy-start.3
  187.2 1.6 pad_maximum_fusion
  188.8 0.0 all-gather.2.cloned.1.call-update
  188.8 0.0 copy-done.3
  188.8 0.1 iota_compare_fusion.3
  188.9 0.7 iota_compare_fusion
  189.6 2.6 broadcast_and_fusion
  192.2 1.3 copy.67
  193.5 78.2 %all-gather.2.cloned.1.call-done = bf16[4,2048,512]{2,1,0:T(8,128)(2,1)} async-done(((bf16[4,512,512]{2,1,0:T(8,128)(2,1)}), bf16[4,2048,512]{2,1,0:T(8,128)(2,1)}) %all-gather.2.cloned.1.call-update) | async-done | bytes 8388624 | tf_op jit(solution)/shard_map/all_gather | solution.py:73
  271.7 5.7 %fusion.44 = (bf16[2,2048,512]{2,1,0:T(8,128)(2,1)}, bf16[2,2048,512]{2,1,0:T(8,128)(2,1)}) fusion(bf16[4,2048,512]{2,1,0:T(8,128)(2,1)} %all-gather.2.cloned.1.call-done), kind=kLoop, calls=%fused_computation.86 | loop fusion | bytes 16777216 | tf_op jit(solution)/shard_map/split | solution.py:72
  277.5 6.3 %copy.68 = bf16[2,2048,512]{1,2,0:T(8,128)(2,1)} copy(bf16[2,2048,512]{2,1,0:T(8,128)(2,1)} %get-tuple-element.5) | data formatting | bytes 8388608 | tf_op jit(solution)/shard_map/split | solution.py:72
  283.8 6.4 %copy.69 = bf16[2,2048,512]{1,2,0:T(8,128)(2,1)} copy(bf16[2,2048,512]{2,1,0:T(8,128)(2,1)} %get-tuple-element.6) | data formatting | bytes 8388608 | tf_op jit(solution)/shard_map/split | solution.py:72
  290.2 0.0 copy-start.1
  290.2 27.1 %fusion = (f32[2,8,512]{2,1,0:T(8,128)S(1)}, f32[2,8,512,2048]{3,2,1,0:T(8,128)}) fusion(pred[2,512,2048]{2,1,0:T(8,128)(4,1)} %broadcast_and_fusion, bf16[2,512,8,64]{1,3,2,0:T(8,128)(2,1)} %bitcast.73, bf16[2,2048,8,64]{1,3,2,0:T(8,128)(2,1)} %bitcast.71), kind=kOutput, calls=%fused_computation.5 | convolution fusion | flops 2197807104 | bytes 74481664 | tf_op jit(solution)/shard_map/bqhd,bkhd->bhqk/dot_general | solution.py:81
  317.3 0.0 copy-done.1
  317.3 22.4 %fusion.1 = f32[2,8,512]{2,1,0:T(8,128)S(1)} fusion(f32[2,8,512,2048]{3,2,1,0:T(8,128)} %get-tuple-element.17, f32[2,8,512]{2,1,0:T(8,128)S(1)} %broadcast_maximum_fusion, pred[2,512,2048]{2,1,0:T(8,128)(4,1)S(1)} %copy-done.1), kind=kLoop, calls=%fused_computation.6 | loop fusion | flops 83877888 | bytes 69271552 | tf_op jit(solution)/shard_map/reduce_sum | solution.py:91
  339.6 27.1 %fusion.16 = bf16[2,512,8,64]{1,3,2,0:T(8,128)(2,1)S(1)} fusion(bf16[2,2048,8,64]{1,3,2,0:T(8,128)(2,1)} %bitcast.75, f32[2,8,512,2048]{3,2,1,0:T(8,128)} %get-tuple-element.17, f32[2,8,512]{2,1,0:T(8,128)S(1)} %broadcast_maximum_fusion, pred[2,512,2048]{2,1,0:T(8,128)(4,1)} %broadcast_and_fusion, f32[2,512,8]{1,2,0:T(8,128)S(1)} %bitcast.85), kind=kOutput, calls=%fused_computation.29 | convolution fusion | flops 2232418304 | bytes 74514432 | tf_op jit(solution)/shard_map/bhqk,bkhd->bhqd/dot_general | solution.py:92
  366.8 0.0 copy-start.4
  366.8 0.0 copy-start.5
  366.8 2.7 fusion.11
  369.5 0.3 copy-done.4
  369.7 0.0 copy-done.5
  369.7 8.3 %fusion.7 = f32[2,512,4096]{2,1,0:T(8,128)} fusion(bf16[512,4096]{1,0:T(8,128)(2,1)S(1)} %copy-done.4, bf16[2,512,512]{1,2,0:T(8,128)(2,1)S(1)} %get-tuple-element.19, f32[512]{0:T(512)S(1)} %copy-done.5, f32[2,512]{1,0:T(2,128)S(1)} %add_rsqrt_fusion), kind=kOutput, calls=%fused_computation.12 | convolution fusion | flops 4297064448 | bytes 22026240 | tf_op jit(solution)/shard_map/bqe,ef->bqf/dot_general | solution.py:108
  378.1 0.0 copy-done
  378.1 8.6 %fusion.14 = bf16[2,512,512]{1,2,0:T(8,128)(2,1)S(1)} fusion(bf16[2,512,512]{1,2,0:T(8,128)(2,1)S(1)} %get-tuple-element.19, bf16[2048,512]{1,0:T(8,128)(2,1)S(1)} %copy-done, f32[2,512,4096]{2,1,0:T(8,128)} %fusion.7), kind=kOutput, calls=%fused_computation.25 | convolution fusion | flops 2161639424 | bytes 20971520 | tf_op jit(solution)/shard_map/bqf,fe->bqe/dot_general | solution.py:111
  386.6 1.3 copy.74
  (16 shorter events, 0.2 us)
Async XLA Ops:
  6.5 371.5 %copy-start = (bf16[2048,512]{1,0:T(8,128)(2,1)S(1)}, bf16[2048,512]{1,0:T(8,128)(2,1)}, u32[]{:S(2)}) copy-start(bf16[2048,512]{1,0:T(8,128)(2,1)} %param.17) | copy-start | bytes 6291460
  94.6 40.9 %all-to-all-start.2 = ((bf16[32,341,128]{2,1,0:T(8,128)(2,1)}), bf16[32,341,128]{2,1,0:T(8,128)(2,1)}, u32[]{:S(2)}, u32[]{:S(2)}) async-start(bf16[32,341,128]{2,1,0:T(8,128)(2,1)} %select_select_fusion), calls=%async_computation.2 | async-start | bytes 5636096 | tf_op jit(solution)/shard_map/all_to_all | solution.py:57
  99.4 172.4 %all-gather.2.cloned.1.call-start = ((), (), s32[]{:S(2)}) async-start(), calls=%async_computation.4 | async-start | bytes 10485760 | tf_op jit(solution)/shard_map/all_gather | solution.py:73
  176.8 5.1 %copy-start.2 = (f32[512]{0:T(512)S(1)}, f32[512]{0:T(512)}, u32[]{:S(2)}) copy-start(f32[512]{0:T(512)} %param.12) | copy-start | bytes 6148
  187.2 1.6 copy-start.3
  290.2 27.1 %copy-start.1 = (pred[2,512,2048]{2,1,0:T(8,128)(4,1)S(1)}, pred[2,512,2048]{2,1,0:T(8,128)(4,1)}, u32[]{:S(2)}) copy-start(pred[2,512,2048]{2,1,0:T(8,128)(4,1)} %broadcast_and_fusion) | copy-start | bytes 6291460
  366.8 3.0 copy-start.4
  366.8 3.0 copy-start.5
Sparse Core Ops, SparseCore 0:
  188.9 82.7 all-gather.1
